TPU v7x, 128 devices: a whole 4x4x4 slice. The times are simulated.
128 devices in a mesh: row: 16 (over y, z), col: 8 (over x, core).
Axes of the slice: x: 4, y: 4, z: 4, core: 2. Of those that a mesh axis runs over, the one named last changes fastest.
Arguments:
- new_dosage: float32 [8192, 1024], P(('col', 'row')), may hold values from 0 to 2
- old_dosage: float32 [32768, 1024], P(('row', 'col')), may hold values from 0 to 2
- grm: bfloat16 [32768, 8192], P('row', 'col'), may hold values from -1.5 to 1.5
- counts: int32 [16], P('col'), may hold values from 256 to 512
- affected: int32 [64, 16], P('row', 'col'), may hold values from 0 to 1, as said below
Outputs:
- updated: bfloat16 [32768, 8192], P('row', 'col')
Inputs may be any that keep to these rules, and one draw needn't show every extreme that they name: `affected`: the density of marked tile pairs differs from one tile of new samples to the next.
All inputs are finite; a program needn't handle non-finite values.
Results may differ from a plain program's by a relative error of at most 0.00115.
Values may be sent and summed in bfloat16 or wider, within the bound.
A program may use at most 128 MiB of HBM per device.

v0:
```python
import jax
import jax.numpy as jnp
from jax import lax
from jax.sharding import Mesh
from jax.sharding import PartitionSpec as P

TILE = 512
ROW = ("row_0", "row_1")
COL = ("col_0", "col_1")
ROW_COL = ("row_0", "row_1", "col_0", "col_1")
COL_ROW = ("col_0", "col_1", "row_0", "row_1")


def one_axis_at_a_time(shard, axes):
    for axis in axes:
        shard = lax.psum(shard, axis)
    return shard


def sent_to_all(shard, axis):
    length = lax.axis_size(axis)
    return lax.all_to_all(
        jnp.broadcast_to(shard[None], (length, *shard.shape)), axis, 0, 0, tiled=True
    )


def joined_along(blocks, dim):
    lengths = list(blocks.shape[1:])
    lengths[dim] *= blocks.shape[0]
    return jnp.moveaxis(blocks, 0, dim).reshape(lengths)


def collect(shard, axis, dim):
    blocks = sent_to_all(shard, axis)
    return joined_along(blocks, dim)


def on_device(new_dosage, old_dosage, grm, counts, affected):
    devices = lax.axis_size(ROW) * lax.axis_size(COL)
    totals = one_axis_at_a_time(jnp.sum(old_dosage, axis=0), ROW_COL)
    doubled = totals / (old_dosage.shape[0] * devices)
    spread = jnp.sqrt(doubled * (1.0 - 0.5 * doubled) + 0.1)
    usable = (jnp.arange(TILE)[None, :] < counts[:, None]).reshape(-1).astype(jnp.float32)
    snp_count = new_dosage.shape[1]
    contract = (((1,), (1,)), ((), ()))
    local_rows = new_dosage.shape[0]
    usable_mine = lax.dynamic_slice_in_dim(usable, lax.axis_index(ROW) * local_rows, local_rows)
    scores_mine = ((new_dosage - doubled) / spread * usable_mine[:, None]).astype(jnp.bfloat16)
    new_scores = collect(scores_mine, ROW, 0)
    old_mine = ((old_dosage - doubled) / spread).astype(jnp.bfloat16)
    product = lax.dot_general(
        lax.all_gather(old_mine, COL, axis=0, tiled=True),
        new_scores,
        contract,
        preferred_element_type=jnp.float32,
    )
    row_count, col_count = product.shape
    scaled = (product / snp_count).reshape(row_count // TILE, TILE, col_count // TILE, TILE)
    masked_update = scaled * affected.astype(jnp.float32)[:, None, :, None]
    return (grm.astype(jnp.float32) + masked_update.reshape(row_count, col_count)).astype(
        jnp.bfloat16
    )


def solution(mesh):
    split = Mesh(mesh.devices.reshape(4, 4, 4, 2), ("row_0", "row_1", "col_0", "col_1"))
    placed = (P(COL_ROW, None), P(ROW_COL, None), P(ROW, COL), P(COL), P(ROW, COL))
    return jax.shard_map(
        on_device, mesh=split, in_specs=placed, out_specs=P(ROW, COL), check_vma=False
    )
```

profile of v0, /device:TPU:0, one launch (start us, length us, event | category | flops | bytes accessed | tf_op | source)
XLA Modules:
  0.0 101.1 jit_solution(6131358367804819225)
XLA Ops:
  6.5 0.0 all-gather.2.cloned.1.call-start
  6.5 1.3 %reduce_sum.9 = f32[1024]{0:T(1024)S(1)} reduce(f32[256,1024]{1,0:T(8,128)} %param.6, f32[]{:T(128)} %constant.12.clone.1), dimensions={0}, to_apply=%region_0.0 | reduce | flops 261120 | bytes 1052676 | tf_op jit(solution)/shard_map/reduce_sum | solution.py:40
  7.8 10.9 %psum.28 = f32[1024]{0:T(1024)S(1)} all-reduce(f32[1024]{0:T(1024)S(1)} %reduce_sum.9), channel_id=1, replica_groups=mesh['row_0'=4,'row_1'=4,'col_0'=4,'col_1'=2] {'row_0'}, use_global_device_ids=true, to_apply=%region_1.0 | all-reduce | flops 1024 | bytes 8192 | tf_op jit(solution)/shard_map/psum | solution.py:16
  18.7 11.8 %psum.29 = f32[1024]{0:T(1024)S(1)} all-reduce(f32[1024]{0:T(1024)S(1)} %psum.28), channel_id=1, replica_groups=mesh['row_0'=4,'row_1'=4,'col_0'=4,'col_1'=2] {'row_1'}, use_global_device_ids=true, to_apply=%region_2.0 | all-reduce | flops 1024 | bytes 8192 | tf_op jit(solution)/shard_map/psum | solution.py:16
  30.5 10.5 %psum.30 = f32[1024]{0:T(1024)S(1)} all-reduce(f32[1024]{0:T(1024)S(1)} %psum.29), channel_id=1, replica_groups=mesh['row_0'=4,'row_1'=4,'col_0'=4,'col_1'=2] {'col_0'}, use_global_device_ids=true, to_apply=%region_3.0 | all-reduce | flops 1024 | bytes 8192 | tf_op jit(solution)/shard_map/psum | solution.py:16
  41.0 2.5 %psum.31 = f32[1024]{0:T(1024)S(1)} all-reduce(f32[1024]{0:T(1024)S(1)} %psum.30), channel_id=1, replica_groups=mesh['row_0'=4,'row_1'=4,'col_0'=4,'col_1'=2] {'col_1'}, use_global_device_ids=true, to_apply=%region_4.0 | all-reduce | flops 1024 | bytes 8192 | tf_op jit(solution)/shard_map/psum | solution.py:16
  43.4 0.0 copy-start
  43.4 2.2 %divide_convert_fusion = bf16[256,1024]{1,0:T(8,128)(2,1)} fusion(f32[256,1024]{1,0:T(8,128)} %param.6, f32[1024]{0:T(1024)S(1)} %get-tuple-element.6, f32[1024]{0:T(1024)S(1)} %get-tuple-element.5), kind=kLoop, calls=%fused_computation.1 | loop fusion | flops 786432 | bytes 1581056 | tf_op jit(solution)/shard_map/convert_element_type | solution.py:50
  45.6 0.0 all-gather.2.cloned.1.call-update
  45.6 0.7 fusion
  46.4 0.1 dynamic_slice.3
  46.5 1.0 %multiply_convert_fusion = bf16[64,1024]{1,0:T(8,128)(2,1)S(1)} fusion(f32[64,1024]{1,0:T(8,128)} %param.5, f32[64]{0:T(128)S(1)} %dynamic_slice.3, f32[1024]{0:T(1024)S(1)} %get-tuple-element.6, f32[1024]{0:T(1024)S(1)} %get-tuple-element.5), kind=kLoop, calls=%fused_computation.2 | loop fusion | flops 262144 | bytes 401664 | tf_op jit(solution)/shard_map/convert_element_type | solution.py:48
  47.5 1.6 %broadcast_in_dim.2 = bf16[16,64,1024]{2,1,0:T(8,128)(2,1)} broadcast(bf16[64,1024]{1,0:T(8,128)(2,1)S(1)} %multiply_convert_fusion), dimensions={1,2} | broadcast | bytes 2228224 | tf_op jit(solution)/shard_map/broadcast_in_dim | solution.py:23
  49.1 3.7 %all-to-all-start = ((bf16[16,64,1024]{2,1,0:T(8,128)(2,1)}), bf16[16,64,1024]{2,1,0:T(8,128)(2,1)S(1)}, u32[]{:S(2)}, u32[]{:S(2)}) async-start(bf16[16,64,1024]{2,1,0:T(8,128)(2,1)} %broadcast_in_dim.2), calls=%async_computation | async-start | bytes 4194304 | tf_op jit(solution)/shard_map/all_to_all | solution.py:22
  52.8 0.0 copy-done
  52.8 0.1 copy.6
  52.9 5.4 %mul.41 = f32[4,512,2,512]{3,2,1,0:T(2,128)} broadcast(f32[4,2]{1,0:T(4,128)S(1)} %copy.6), dimensions={0,2} | broadcast | bytes 8388640 | tf_op jit(solution)/shard_map/mul | solution.py:59
  58.4 8.9 %copy.8 = f32[256,8,2,512]{3,1,2,0:T(8,128)} copy(f32[256,8,2,512]{3,2,1,0:T(2,128)} %bitcast.9) | data formatting | bytes 16777216
  67.2 16.3 %all-to-all-done = bf16[16,64,1024]{2,1,0:T(8,128)(2,1)S(1)} async-done(((bf16[16,64,1024]{2,1,0:T(8,128)(2,1)}), bf16[16,64,1024]{2,1,0:T(8,128)(2,1)S(1)}, u32[]{:S(2)}, u32[]{:S(2)}) %all-to-all-start) | async-done | bytes 2097184 | tf_op jit(solution)/shard_map/all_to_all | solution.py:22
  83.5 0.0 all-gather.2.cloned.1.call-done
  83.5 10.8 %add_convert_fusion = bf16[2048,1024]{1,0:T(8,128)(2,1)} fusion(f32[2048,1024]{1,0:T(8,128)} %bitcast.10, bf16[2048,1024]{1,0:T(8,128)(2,1)} %param.7, bf16[2048,1024]{1,0:T(8,128)(2,1)} %all-gather.2.cloned.1.call-done, bf16[1024,1024]{1,0:T(8,128)(2,1)S(1)} %bitcast.11), kind=kOutput, calls=%fused_computation | convolution fusion | flops 4305453056 | bytes 23068672 | tf_op jit(solution)/shard_map/dot_general | solution.py:51
  (3 shorter events, 0.0 us)
Async XLA Ops:
  6.5 77.0 %all-gather.2.cloned.1.call-start = ((), (), s32[]{:S(2)}) async-start(), calls=%async_computation.1 | async-start | bytes 4718592 | tf_op jit(solution)/shard_map/all_gather | solution.py:52
  43.4 9.4 %copy-start = (s32[4,2]{0,1:T(2,128)S(1)}, s32[4,2]{0,1:T(2,128)}, u32[]{:S(2)}) copy-start(s32[4,2]{0,1:T(2,128)} %param.9) | copy-start | bytes 100
  49.1 34.4 %all-to-all-start = ((bf16[16,64,1024]{2,1,0:T(8,128)(2,1)}), bf16[16,64,1024]{2,1,0:T(8,128)(2,1)S(1)}, u32[]{:S(2)}, u32[]{:S(2)}) async-start(bf16[16,64,1024]{2,1,0:T(8,128)(2,1)} %broadcast_in_dim.2), calls=%async_computation | async-start | bytes 4194304 | tf_op jit(solution)/shard_map/all_to_all | solution.py:22
Sparse Core Ops, SparseCore 0:
  45.8 26.6 all-gather.1
where the time goes:
time: 101 us
  blocking collectives  35.6 us (35%)
  waiting for transfers between devices  16.3 us (16%)
  local copies, waits for them, and re-layouts  16.1 us (16%)
  between operations  13.4 us (13%)
  matrix products  10.8 us (11%)
  other arithmetic  5.26 us (5%)
  starting transfers between devices  3.74 us (4%)
    psum x4, blocking collectives, one_axis_at_a_time(): shard = lax.psum(shard, axis)  35.6 us
    all_to_all x1, waiting for transfers between devices, sent_to_all(): lax.all_to_all(jnp.broadcast_to(shard[None], (length, *shard.shape)), axi...  16.3 us
    dot_general x1, matrix products, on_device(): lax.dot_general(lax.all_gather(old_mine, COL, axis=0, tiled=True), new_sc...  10.8 us
    unnamed x4, local copies, waits for them, and re-layouts  8.86 us
    mul x1, local copies, waits for them, and re-layouts, on_device(): masked_update = scaled * affected.astype(jnp.float32)[:, None, :, None]  5.44 us
    all_to_all x1, starting transfers between devices, sent_to_all(): lax.all_to_all(jnp.broadcast_to(shard[None], (length, *shard.shape)), axi...  3.74 us
    convert_element_type x1, other arithmetic, on_device(): old_mine = ((old_dosage - doubled) / spread).astype(jnp.bfloat16)  2.18 us
  transfers between devices with their start and end apart: 2, of which 1 were waited for; matrix products, arithmetic and copies ran while one was open for 18% of the time, Pallas kernels for 0%

commit v1 on v0

--- a/solution.py
+++ b/solution.py
@@ -13,7 +13,7 @@
 
 def one_axis_at_a_time(shard, axes):
     for axis in axes:
-        shard = lax.psum(shard, axis)
+        shard = jnp.sum(lax.all_gather(shard, axis), axis=0)
     return shard
 
 

time: 101 us -> 109 us (1.079)
  blocking collectives: 35.6 us -> 40 us
  starting transfers between devices: 3.74 us -> 6.14 us
    all_gather x0 -> x4, blocking collectives: none -> 40 us  [one_axis_at_a_time(): shard = jnp.sum(lax.all_gather(shard, axis), axis=0)]
    psum x4 -> x0, blocking collectives: 35.6 us -> none  [one_axis_at_a_time(): shard = lax.psum(shard, axis)]
    all_to_all x1, starting transfers between devices: 3.74 us -> 6.14 us  [sent_to_all(): lax.all_to_all(jnp.broadcast_to(shard[None], (length, *shard.shape)), axi...]
  transfers between devices with their start and end apart: 2 -> 2, of which waited for: 1 -> 1; matrix products, arithmetic and copies ran while one was open for 18% -> 16% of each run, Pallas kernels for 0% -> 0%
where the time goes in v1:
time: 109 us
  blocking collectives  40 us (37%)
  waiting for transfers between devices  16.8 us (15%)
  local copies, waits for them, and re-layouts  16.1 us (15%)
  between operations  13.5 us (12%)
  matrix products  10.8 us (10%)
  starting transfers between devices  6.14 us (6%)
  other arithmetic  5.31 us (5%)
    all_gather x4, blocking collectives, one_axis_at_a_time(): shard = jnp.sum(lax.all_gather(shard, axis), axis=0)  40 us
    all_to_all x1, waiting for transfers between devices, sent_to_all(): lax.all_to_all(jnp.broadcast_to(shard[None], (length, *shard.shape)), axi...  16.8 us
    dot_general x1, matrix products, on_device(): lax.dot_general(lax.all_gather(old_mine, COL, axis=0, tiled=True), new_sc...  10.8 us
    unnamed x4, local copies, waits for them, and re-layouts  8.87 us
    all_to_all x1, starting transfers between devices, sent_to_all(): lax.all_to_all(jnp.broadcast_to(shard[None], (length, *shard.shape)), axi...  6.14 us
    mul x1, local copies, waits for them, and re-layouts, on_device(): masked_update = scaled * affected.astype(jnp.float32)[:, None, :, None]  5.44 us
  transfers between devices with their start and end apart: 2, of which 1 were waited for; matrix products, arithmetic and copies ran while one was open for 16% of the time, Pallas kernels for 0%

profile of v1, /device:TPU:0, one launch (start us, length us, event | category | flops | bytes accessed | tf_op | source)
XLA Modules:
  0.0 108.6 jit_solution(12491476773661567551)
XLA Ops:
  6.5 0.0 all-gather.6.cloned.1.call-start
  6.5 1.3 %reduce_sum.45 = f32[1024]{0:T(1024)S(1)} reduce(f32[256,1024]{1,0:T(8,128)} %param.6, f32[]{:T(128)} %constant.12.clone.1), dimensions={0}, to_apply=%region_0.0 | reduce | flops 261120 | bytes 1052676 | tf_op jit(solution)/shard_map/reduce_sum | solution.py:40
  7.8 12.6 %all-gather = f32[4096]{0:T(1024)S(1)} all-gather(f32[1024]{0:T(1024)S(1)} %reduce_sum.45), channel_id=2, replica_groups=mesh['row_0'=4,'row_1'=4,'col_0'=4,'col_1'=2] {'row_0'}, dimensions={0}, use_global_device_ids=true | all-gather | bytes 20480 | tf_op jit(solution)/shard_map/all_gather | solution.py:16
  20.5 13.2 %all-gather.1 = f32[4096]{0:T(1024)S(1)} all-gather(f32[1024]{0:T(1024)S(1)} %reduce_sum.46), channel_id=3, replica_groups=mesh['row_0'=4,'row_1'=4,'col_0'=4,'col_1'=2] {'row_1'}, dimensions={0}, use_global_device_ids=true | all-gather | bytes 20480 | tf_op jit(solution)/shard_map/all_gather | solution.py:16
  33.8 12.4 %all-gather.2 = f32[4096]{0:T(1024)S(1)} all-gather(f32[1024]{0:T(1024)S(1)} %reduce_sum.47), channel_id=4, replica_groups=mesh['row_0'=4,'row_1'=4,'col_0'=4,'col_1'=2] {'col_0'}, dimensions={0}, use_global_device_ids=true | all-gather | bytes 20480 | tf_op jit(solution)/shard_map/all_gather | solution.py:16
  46.2 1.8 %all-gather.3 = f32[2048]{0:T(1024)S(1)} all-gather(f32[1024]{0:T(1024)S(1)} %reduce_sum.48), channel_id=5, replica_groups=mesh['row_0'=4,'row_1'=4,'col_0'=4,'col_1'=2] {'col_1'}, dimensions={0}, use_global_device_ids=true | all-gather | bytes 12288 | tf_op jit(solution)/shard_map/all_gather | solution.py:16
  48.0 0.0 copy-start
  48.0 2.2 %divide_convert_fusion = bf16[256,1024]{1,0:T(8,128)(2,1)} fusion(f32[256,1024]{1,0:T(8,128)} %param.6, f32[1024]{0:T(1024)S(1)} %get-tuple-element.6, f32[1024]{0:T(1024)S(1)} %get-tuple-element.5), kind=kLoop, calls=%fused_computation.1 | loop fusion | flops 786432 | bytes 1581056 | tf_op jit(solution)/shard_map/convert_element_type | solution.py:50
  50.2 0.0 all-gather.6.cloned.1.call-update
  50.2 0.7 fusion
  51.0 0.1 dynamic_slice.3
  51.1 1.0 multiply_convert_fusion
  52.1 1.6 %broadcast_in_dim.2 = bf16[16,64,1024]{2,1,0:T(8,128)(2,1)} broadcast(bf16[64,1024]{1,0:T(8,128)(2,1)S(1)} %multiply_convert_fusion), dimensions={1,2} | broadcast | bytes 2228224 | tf_op jit(solution)/shard_map/broadcast_in_dim | solution.py:23
  53.7 6.1 %all-to-all-start = ((bf16[16,64,1024]{2,1,0:T(8,128)(2,1)}), bf16[16,64,1024]{2,1,0:T(8,128)(2,1)S(1)}, u32[]{:S(2)}, u32[]{:S(2)}) async-start(bf16[16,64,1024]{2,1,0:T(8,128)(2,1)} %broadcast_in_dim.2), calls=%async_computation | async-start | bytes 4194304 | tf_op jit(solution)/shard_map/all_to_all | solution.py:22
  59.8 0.0 copy-done
  59.8 0.1 copy.8
  59.9 5.4 %mul.49 = f32[4,512,2,512]{3,2,1,0:T(2,128)} broadcast(f32[4,2]{1,0:T(4,128)S(1)} %copy.8), dimensions={0,2} | broadcast | bytes 8388640 | tf_op jit(solution)/shard_map/mul | solution.py:59
  65.4 8.9 %copy.10 = f32[256,8,2,512]{3,1,2,0:T(8,128)} copy(f32[256,8,2,512]{3,2,1,0:T(2,128)} %bitcast.9) | data formatting | bytes 16777216
  74.2 16.8 %all-to-all-done = bf16[16,64,1024]{2,1,0:T(8,128)(2,1)S(1)} async-done(((bf16[16,64,1024]{2,1,0:T(8,128)(2,1)}), bf16[16,64,1024]{2,1,0:T(8,128)(2,1)S(1)}, u32[]{:S(2)}, u32[]{:S(2)}) %all-to-all-start) | async-done | bytes 2097184 | tf_op jit(solution)/shard_map/all_to_all | solution.py:22
  91.0 0.0 all-gather.6.cloned.1.call-done
  91.0 10.8 %add_convert_fusion = bf16[2048,1024]{1,0:T(8,128)(2,1)} fusion(f32[2048,1024]{1,0:T(8,128)} %bitcast.10, bf16[2048,1024]{1,0:T(8,128)(2,1)} %param.7, bf16[2048,1024]{1,0:T(8,128)(2,1)} %all-gather.6.cloned.1.call-done, bf16[1024,1024]{1,0:T(8,128)(2,1)S(1)} %bitcast.11), kind=kOutput, calls=%fused_computation | convolution fusion | flops 4305453056 | bytes 23068672 | tf_op jit(solution)/shard_map/dot_general | solution.py:51
  (11 shorter events, 0.1 us)
Async XLA Ops:
  6.5 84.5 %all-gather.6.cloned.1.call-start = ((), (), s32[]{:S(2)}) async-start(), calls=%async_computation.1 | async-start | bytes 4718592 | tf_op jit(solution)/shard_map/all_gather | solution.py:52
  48.0 11.8 %copy-start = (s32[4,2]{0,1:T(2,128)S(1)}, s32[4,2]{0,1:T(2,128)}, u32[]{:S(2)}) copy-start(s32[4,2]{0,1:T(2,128)} %param.9) | copy-start | bytes 100
  53.7 37.3 %all-to-all-start = ((bf16[16,64,1024]{2,1,0:T(8,128)(2,1)}), bf16[16,64,1024]{2,1,0:T(8,128)(2,1)S(1)}, u32[]{:S(2)}, u32[]{:S(2)}) async-start(bf16[16,64,1024]{2,1,0:T(8,128)(2,1)} %broadcast_in_dim.2), calls=%async_computation | async-start | bytes 4194304 | tf_op jit(solution)/shard_map/all_to_all | solution.py:22
Sparse Core Ops, SparseCore 0:
  50.4 31.8 all-gather.5
